TPU v7x, 128 devices: a whole 4x4x4 slice. The times are simulated.
128 devices in a mesh: dp: 16 (over z, x), expert: 8 (over y, core).
Axes of the slice: x: 4, y: 4, z: 4, core: 2. Of those that a mesh axis runs over, the one named last changes fastest.
Arguments:
- tokens: bfloat16 [16384, 2048], P(('dp', 'expert')), may hold values from -6 to 6
- cotangent: bfloat16 [16384, 2048], P(('dp', 'expert')), may hold values from -6 to 6
- expert_ids: int32 [16384, 2], P(('dp', 'expert')), may hold values from 0 to 7, all different within a row; in each aligned block of 128 rows (0 to 127, 128 to 255, ...) at most 36 rows name the same one
- route_share: float32 [16384], P(('dp', 'expert')), may hold values from 0.5 to 0.95
- gate_proj: bfloat16 [8, 7168, 2048], P('expert', 'dp'), may hold values from -0.125 to 0.125
- up_proj: bfloat16 [8, 7168, 2048], P('expert', 'dp'), may hold values from -0.125 to 0.125
- down_anchor: float32 [8, 7168, 2048], P('expert', 'dp'), may hold values from -0.12 to 0.12
- down_average: float32 [8, 7168, 2048], P('expert', 'dp'), may hold values from -0.12 to 0.12
- down_moment: float32 [8, 7168, 2048], P('expert', 'dp'), may hold values from 0.002 to 0.05
Outputs:
- new_anchor: float32 [8, 7168, 2048], P('expert', 'dp')
- new_average: float32 [8, 7168, 2048], P('expert', 'dp')
- new_moment: float32 [8, 7168, 2048], P('expert', 'dp')
Inputs may be any that keep to these rules, and one draw needn't show every extreme that they name: `expert_ids`: the two ids of a token differ. The rows of one device name any expert at most 36 times, and in every draw some device names some expert exactly 36 times.
All inputs are finite; a program needn't handle non-finite values.
Results may differ from a plain program's by a relative error of at most 0.0043.
Values may be sent and summed in bfloat16 or wider, within the bound.
A program may use at most 192 MiB of HBM per device.

v0:
```python
import jax
import jax.numpy as jnp
from jax import lax
from jax.sharding import PartitionSpec as P

FF = 7168
TOPK = 2


beta_one = 0.9
beta_two = 0.95
learn_rate = 0.05
decay_rate = 0.1
step_count = 4.0
epsilon = 1e-08


def expert_terms(pieces, weight_gate, weight_up):
    rows_in, gated_rows = pieces
    gate_act = lax.dot_general(
        rows_in, weight_gate, (((1,), (1,)), ((), ())), preferred_element_type=jnp.float32
    )
    up_act = lax.dot_general(
        rows_in, weight_up, (((1,), (1,)), ((), ())), preferred_element_type=jnp.float32
    )
    hidden = (jax.nn.silu(gate_act) * up_act).astype(jnp.bfloat16)
    return lax.dot_general(
        hidden, gated_rows, (((0,), (0,)), ((), ())), preferred_element_type=jnp.float32
    )


def shards(
    tokens,
    cotangent,
    expert_ids,
    route_share,
    gate_proj,
    up_proj,
    down_anchor,
    down_average,
    down_moment,
):
    experts_all = lax.axis_size("expert")
    tok_rows = tokens.shape[0]
    width = tokens.shape[1]
    capacity = tok_rows * TOPK // experts_all * 9 // 8
    slots = experts_all * capacity
    shares = jnp.stack([route_share, 1.0 - route_share], axis=1)
    expert_range = jnp.arange(experts_all, dtype=jnp.int32)
    flat_ids = expert_ids.reshape(-1)
    onehot_routes = (flat_ids[:, None] == expert_range[None, :]).astype(jnp.int32)
    earlier = jnp.cumsum(onehot_routes, axis=0) - onehot_routes
    slot_of = jnp.sum(earlier * onehot_routes, axis=1)
    target = (flat_ids * capacity + slot_of).reshape(tok_rows, TOPK)
    slot_range = jnp.arange(slots, dtype=jnp.int32)
    placed = target[None, :, :] == slot_range[:, None, None]
    picker = jnp.sum(placed.astype(jnp.float32), axis=2).astype(jnp.bfloat16)
    slot_share = jnp.sum(jnp.where(placed, shares[None, :, :], 0.0), axis=(1, 2))
    send_rows = jnp.dot(picker, tokens, preferred_element_type=jnp.float32).astype(jnp.bfloat16)
    send_grad = (
        slot_share[:, None] * jnp.dot(picker, cotangent, preferred_element_type=jnp.float32)
    ).astype(jnp.bfloat16)
    weight_gate = gate_proj[0]
    weight_up = up_proj[0]
    arrived = (
        lax.all_to_all(
            send_rows.reshape(experts_all, capacity, width),
            "expert",
            split_axis=0,
            concat_axis=0,
            tiled=True,
        ),
        lax.all_to_all(
            send_grad.reshape(experts_all, capacity, width),
            "expert",
            split_axis=0,
            concat_axis=0,
            tiled=True,
        ),
    )
    rows_here = arrived[0].reshape(slots, width)
    grad_here = arrived[1].reshape(slots, width)
    gradient = expert_terms(
        (
            lax.all_gather(rows_here, "dp", axis=0, tiled=True),
            lax.all_gather(grad_here, "dp", axis=0, tiled=True),
        ),
        weight_gate,
        weight_up,
    )
    gradient = gradient[None] * FF ** (-0.5)
    bias_two = 1.0 - beta_two**step_count
    eval_point = (1.0 - beta_one) * down_anchor + beta_one * down_average
    second_moment = beta_two * down_moment + (1.0 - beta_two) * gradient * gradient
    update_dir = gradient / (jnp.sqrt(second_moment / bias_two) + epsilon) + decay_rate * eval_point
    new_anchor = down_anchor - learn_rate * update_dir
    new_average = (1.0 - 1.0 / step_count) * down_average + 1.0 / step_count * new_anchor
    return (new_anchor, new_average, second_moment)


def solution(mesh):
    placed = (
        P(("dp", "expert"), None),
        P(("dp", "expert"), None),
        P(("dp", "expert"), None),
        P(("dp", "expert")),
        P("expert", "dp", None),
        P("expert", "dp", None),
        P("expert", "dp", None),
        P("expert", "dp", None),
        P("expert", "dp", None),
    )
    return jax.shard_map(
        shards,
        mesh=mesh,
        in_specs=placed,
        out_specs=(P("expert", "dp", None), P("expert", "dp", None), P("expert", "dp", None)),
        check_vma=False,
    )
```

profile of v0, /device:TPU:1, one launch (start us, length us, event | category | flops | bytes accessed | tf_op | source)
XLA Modules:
  0.0 330.5 jit_solution(17586150212628106540)
XLA Ops:
  7.2 0.0 copy-start
  7.2 0.0 all-gather.3.cloned.1.call-start
  7.2 0.9 copy.24
  8.1 0.1 eq.42
  8.3 0.1 eq.38
  8.4 0.7 subtract_bitcast_fusion
  9.1 0.6 reduce-window.6
  9.7 0.2 slice_reduce_fusion
  9.9 0.1 fusion.11
  10.0 0.1 reduce_sum.30
  10.2 0.1 copy.26
  10.2 0.7 multiply_add_fusion.1
  10.9 0.7 pad_maximum_fusion
  11.6 0.2 select_reduce_fusion
  11.7 2.5 convolution_convert_fusion
  14.2 1.4 reshape.48
  15.6 23.6 %all_to_all.10 = bf16[8,36,2048]{2,1,0:T(8,128)(2,1)} all-to-all(bf16[8,36,2048]{2,1,0:T(8,128)(2,1)S(1)} %reshape.48), channel_id=1, replica_groups=mesh['dp'=16,'expert'=8] {'expert'}, dimensions={0} | all-to-all | bytes 2359296 | tf_op jit(solution)/shard_map/all_to_all | solution.py:66
  39.2 0.0 copy-start.1
  39.2 2.3 reshape.49
  41.5 0.0 all-gather.3.cloned.1.call-update
  41.5 0.0 all-gather.5.cloned.1.call-start
  41.6 0.0 copy-done.1
  41.6 1.5 fusion.4
  43.1 1.4 reshape.50
  44.5 21.9 %all_to_all.11 = bf16[8,36,2048]{2,1,0:T(8,128)(2,1)} all-to-all(bf16[8,36,2048]{2,1,0:T(8,128)(2,1)S(1)} %reshape.50), channel_id=1, replica_groups=mesh['dp'=16,'expert'=8] {'expert'}, dimensions={0} | all-to-all | bytes 2359296 | tf_op jit(solution)/shard_map/all_to_all | solution.py:73
  66.4 2.2 reshape.51
  68.6 0.0 all-gather.5.cloned.1.call-update
  68.6 95.7 %all-gather.3.cloned.1.call-done = bf16[4608,2048]{1,0:T(8,128)(2,1)} async-done(((bf16[288,2048]{1,0:T(8,128)(2,1)}), bf16[4608,2048]{1,0:T(8,128)(2,1)}) %all-gather.3.cloned.1.call-update) | async-done | bytes 18874384 | tf_op jit(solution)/shard_map/all_gather | solution.py:85
  164.3 15.2 %fusion.6 = f32[4608,448]{0,1:T(8,128)} fusion(bf16[4608,2048]{1,0:T(8,128)(2,1)} %all-gather.3.cloned.1.call-done, bf16[1,448,2048]{2,1,0:T(8,128)(2,1)} %param.13), kind=kOutput, calls=%fused_computation.12 | convolution fusion | flops 8455716864 | bytes 28966912 | tf_op jit(solution)/shard_map/dot_general | solution.py:20
  179.5 109.2 %all-gather.5.cloned.1.call-done = bf16[4608,2048]{1,0:T(8,128)(2,1)} async-done(((bf16[288,2048]{1,0:T(8,128)(2,1)}), bf16[4608,2048]{1,0:T(8,128)(2,1)}) %all-gather.5.cloned.1.call-update) | async-done | bytes 18874384 | tf_op jit(solution)/shard_map/all_gather | solution.py:86
  288.7 0.0 copy-done
  288.7 34.9 %multiply_add_fusion = (f32[1,448,2048]{2,1,0:T(8,128)}, f32[1,448,2048]{2,1,0:T(8,128)}, f32[1,448,2048]{2,1,0:T(8,128)}) fusion(f32[1,448,2048]{2,1,0:T(8,128)} %param.16, f32[1,448,2048]{2,1,0:T(8,128)} %param.15, f32[1,448,2048]{2,1,0:T(8,128)} %param.17, bf16[4608,2048]{1,0:T(8,128)(2,1)} %all-gather.5.cloned.1.call-done, ...), kind=kOutput, calls=%fused_computation.7 | convolution fusion | flops 16940335104 | bytes 69861376 | tf_op jit(solution)/shard_map/dot_general | solution.py:27
  (3 shorter events, 0.0 us)
Async XLA Ops:
  7.2 281.5 %copy-start = (bf16[1,448,2048]{2,1,0:T(8,128)(2,1)S(1)}, bf16[1,448,2048]{2,1,0:T(8,128)(2,1)}, u32[]{:S(2)}) copy-start(bf16[1,448,2048]{2,1,0:T(8,128)(2,1)} %param.14) | copy-start | bytes 5505028
  7.2 157.1 %all-gather.3.cloned.1.call-start = ((), (), s32[]{:S(2)}) async-start(), calls=%async_computation.2 | async-start | bytes 20054016 | tf_op jit(solution)/shard_map/all_gather | solution.py:85
  39.2 2.4 copy-start.1
  41.5 247.1 %all-gather.5.cloned.1.call-start = ((), (), s32[]{:S(2)}) async-start(), calls=%async_computation.3 | async-start | bytes 20054016 | tf_op jit(solution)/shard_map/all_gather | solution.py:86
Sparse Core Ops, SparseCore 0:
  41.7 122.6 all-gather.2
  167.0 121.6 all-gather.4
where the time goes:
time: 331 us; the launch traced here: 330 us
  waiting for transfers between devices  205 us (62%)
  matrix products  54.1 us (16%)
  blocking collectives  45.5 us (14%)
  between operations  14.1 us (4%)
  local copies, waits for them, and re-layouts  8.88 us (3%)
    all_gather x1, waiting for transfers between devices, shards(): lax.all_gather(grad_here, 'dp', axis=0, tiled=True)  109 us
    all_gather x1, waiting for transfers between devices, shards(): lax.all_gather(rows_here, 'dp', axis=0, tiled=True)  95.7 us
    dot_general x1, matrix products, expert_terms(): lax.dot_general(hidden, gated_rows, (((0,), (0,)), ((), ())), preferred_e...  34.9 us
    all_to_all x1, blocking collectives, shards(): lax.all_to_all(send_rows.reshape(experts_all, capacity, width), 'expert',...  23.6 us
    all_to_all x1, blocking collectives, shards(): lax.all_to_all(send_grad.reshape(experts_all, capacity, width), 'expert',...  21.9 us
    dot_general x1, matrix products, expert_terms(): lax.dot_general(rows_in, weight_gate, (((1,), (1,)), ((), ())), preferred...  15.2 us
  transfers between devices with their start and end apart: 2, of which 2 were waited for; matrix products, arithmetic and copies ran while one was open for 6% of the time, Pallas kernels for 0%

commit v1 on v0

--- a/solution.py
+++ b/solution.py
@@ -6,7 +6,6 @@
 FF = 7168
 TOPK = 2
 
-
 beta_one = 0.9
 beta_two = 0.95
 learn_rate = 0.05
@@ -14,19 +13,25 @@
 step_count = 4.0
 epsilon = 1e-08
 
+BOTH = ("dp", "expert")
+SIDE = 4
 
-def expert_terms(pieces, weight_gate, weight_up):
-    rows_in, gated_rows = pieces
-    gate_act = lax.dot_general(
-        rows_in, weight_gate, (((1,), (1,)), ((), ())), preferred_element_type=jnp.float32
-    )
-    up_act = lax.dot_general(
-        rows_in, weight_up, (((1,), (1,)), ((), ())), preferred_element_type=jnp.float32
-    )
-    hidden = (jax.nn.silu(gate_act) * up_act).astype(jnp.bfloat16)
-    return lax.dot_general(
-        hidden, gated_rows, (((0,), (0,)), ((), ())), preferred_element_type=jnp.float32
-    )
+
+def lines(along_x_for_even):
+    groups = []
+    for expert in range(8):
+        along_x = (expert % 2 == 0) == along_x_for_even
+        for fixed in range(SIDE):
+            if along_x:
+                dps = [fixed * SIDE + i for i in range(SIDE)]
+            else:
+                dps = [i * SIDE + fixed for i in range(SIDE)]
+            groups.append([dp * 8 + expert for dp in dps])
+    return groups
+
+
+WEIGHT_LINES = lines(True)
+ROW_LINES = lines(False)
 
 
 def shards(
@@ -45,6 +50,8 @@
     width = tokens.shape[1]
     capacity = tok_rows * TOPK // experts_all * 9 // 8
     slots = experts_all * capacity
+    weight_gate = lax.all_gather(gate_proj[0], BOTH, axis=0, tiled=True, axis_index_groups=WEIGHT_LINES)
+    weight_up = lax.all_gather(up_proj[0], BOTH, axis=0, tiled=True, axis_index_groups=WEIGHT_LINES)
     shares = jnp.stack([route_share, 1.0 - route_share], axis=1)
     expert_range = jnp.arange(experts_all, dtype=jnp.int32)
     flat_ids = expert_ids.reshape(-1)
@@ -60,34 +67,29 @@
     send_grad = (
         slot_share[:, None] * jnp.dot(picker, cotangent, preferred_element_type=jnp.float32)
     ).astype(jnp.bfloat16)
-    weight_gate = gate_proj[0]
-    weight_up = up_proj[0]
-    arrived = (
-        lax.all_to_all(
-            send_rows.reshape(experts_all, capacity, width),
-            "expert",
-            split_axis=0,
-            concat_axis=0,
-            tiled=True,
-        ),
-        lax.all_to_all(
-            send_grad.reshape(experts_all, capacity, width),
-            "expert",
-            split_axis=0,
-            concat_axis=0,
-            tiled=True,
-        ),
+    rows_here = lax.all_to_all(
+        send_rows.reshape(experts_all, capacity, width), "expert",
+        split_axis=0, concat_axis=0, tiled=True,
+    ).reshape(slots, width)
+    grad_here = lax.all_to_all(
+        send_grad.reshape(experts_all, capacity, width), "expert",
+        split_axis=0, concat_axis=0, tiled=True,
+    ).reshape(slots, width)
+    rows_all = lax.all_gather(rows_here, BOTH, axis=0, tiled=True, axis_index_groups=ROW_LINES)
+    grad_all = lax.all_gather(grad_here, BOTH, axis=0, tiled=True, axis_index_groups=ROW_LINES)
+    gate_act = lax.dot_general(
+        rows_all, weight_gate, (((1,), (1,)), ((), ())), preferred_element_type=jnp.float32
     )
-    rows_here = arrived[0].reshape(slots, width)
-    grad_here = arrived[1].reshape(slots, width)
-    gradient = expert_terms(
-        (
-            lax.all_gather(rows_here, "dp", axis=0, tiled=True),
-            lax.all_gather(grad_here, "dp", axis=0, tiled=True),
-        ),
-        weight_gate,
-        weight_up,
+    up_act = lax.dot_general(
+        rows_all, weight_up, (((1,), (1,)), ((), ())), preferred_element_type=jnp.float32
     )
+    hidden = (jax.nn.silu(gate_act) * up_act).astype(jnp.bfloat16)
+    part = lax.dot_general(
+        hidden, grad_all, (((0,), (0,)), ((), ())), preferred_element_type=jnp.float32
+    ).astype(jnp.bfloat16)
+    gradient = lax.psum_scatter(
+        part, BOTH, scatter_dimension=0, tiled=True, axis_index_groups=WEIGHT_LINES
+    ).astype(jnp.float32)
     gradient = gradient[None] * FF ** (-0.5)
     bias_two = 1.0 - beta_two**step_count
     eval_point = (1.0 - beta_one) * down_anchor + beta_one * down_average

time: 331 us -> 293 us (0.89)
  waiting for transfers between devices: 205 us -> 173 us
  matrix products: 54.1 us -> 43.8 us
  other arithmetic: 2.88 us -> 12.8 us
  local copies, waits for them, and re-layouts: 8.88 us -> 4.37 us
    all_gather x2 -> x4, waiting for transfers between devices: 205 us -> 127 us  [the longest x1 47.7 us: shards(): lax.all_gather(gate_proj[0], BOTH, axis=0, tiled=True, axis_index_groups=...]
    reduce_scatter x0 -> x1, waiting for transfers between devices: none -> 44.5 us  [shards(): lax.psum_scatter(part, BOTH, scatter_dimension=0, tiled=True, axis_index_...]
    add x0 -> x1, other arithmetic: none -> 9.94 us  [shards(): (1.0 - 1.0 / step_count) * down_average + 1.0 / step_count * new_anchor]
    dot_general x2, matrix products: 50.1 us -> 42.9 us  [the longest x1 28.2 us: shards(): lax.dot_general(hidden, grad_all, (((0,), (0,)), ((), ())), preferred_ele...]
  transfers between devices with their start and end apart: 2 -> 5, of which waited for: 2 -> 5; matrix products, arithmetic and copies ran while one was open for 6% -> 6% of each run, Pallas kernels for 0% -> 0%
where the time goes in v1:
time: 293 us
  waiting for transfers between devices  173 us (59%)
  blocking collectives  44.9 us (15%)
  matrix products  43.8 us (15%)
  between operations  13.9 us (5%)
  other arithmetic  12.8 us (4%)
  local copies, waits for them, and re-layouts  4.37 us (1%)
    all_gather x1, waiting for transfers between devices, shards(): lax.all_gather(gate_proj[0], BOTH, axis=0, tiled=True, axis_index_groups=...  47.7 us
    all_gather x1, waiting for transfers between devices, shards(): lax.all_gather(up_proj[0], BOTH, axis=0, tiled=True, axis_index_groups=WE...  47.6 us
    reduce_scatter x1, waiting for transfers between devices, shards(): lax.psum_scatter(part, BOTH, scatter_dimension=0, tiled=True, axis_index_...  44.5 us
    dot_general x1, matrix products, shards(): lax.dot_general(hidden, grad_all, (((0,), (0,)), ((), ())), preferred_ele...  28.2 us
    all_to_all x1, blocking collectives, shards(): lax.all_to_all(send_rows.reshape(experts_all, capacity, width), 'expert',...  23.6 us
    all_gather x1, waiting for transfers between devices, shards(): lax.all_gather(grad_here, BOTH, axis=0, tiled=True, axis_index_groups=ROW...  22.1 us
    all_to_all x1, blocking collectives, shards(): lax.all_to_all(send_grad.reshape(experts_all, capacity, width), 'expert',...  21.3 us
    dot_general x1, matrix products, shards(): lax.dot_general(rows_all, weight_gate, (((1,), (1,)), ((), ())), preferre...  14.7 us
  transfers between devices with their start and end apart: 5, of which 5 were waited for; matrix products, arithmetic and copies ran while one was open for 6% of the time, Pallas kernels for 0%

profile of v1, /device:TPU:1, one launch (start us, length us, event | category | flops | bytes accessed | tf_op | source)
XLA Modules:
  0.0 293.2 jit_solution(16474653333690841074)
XLA Ops:
  7.2 0.0 copy-start
  7.2 0.0 all-gather.7.cloned.1.call-start
  7.2 0.8 copy.24
  8.1 0.1 eq.42
  8.2 0.1 eq.38
  8.3 0.7 subtract_bitcast_fusion
  9.0 0.6 reduce-window.6
  9.6 0.2 slice_reduce_fusion
  9.8 0.1 fusion.20
  9.9 0.1 reduce_sum.30
  10.1 0.1 copy.26
  10.1 0.7 multiply_add_fusion.1
  10.8 0.7 pad_maximum_fusion
  11.5 0.2 convert_reduce_fusion
  11.7 0.0 copy-done
  11.7 0.5 convolution_convert_fusion
  12.1 0.3 reshape.48
  12.4 0.0 copy-start.2
  12.4 23.6 %all_to_all.10 = bf16[8,36,2048]{2,1,0:T(8,128)(2,1)S(1)} all-to-all(bf16[8,36,2048]{2,1,0:T(8,128)(2,1)S(1)} %reshape.48), channel_id=1, replica_groups=mesh['dp'=16,'expert'=8] {'expert'}, dimensions={0} | all-to-all | bytes 2359296 | tf_op jit(solution)/shard_map/all_to_all | solution.py:70
  36.1 1.1 reshape.49
  37.2 0.0 all-gather.7.cloned.1.call-update
  37.2 0.0 all-gather.11.cloned.1.call-start
  37.3 0.7 all-gather.11.cloned.1.call-update
  38.0 0.0 all-gather.9.cloned.1.call-start
  38.0 0.0 copy-done.2
  38.0 0.5 fusion.16
  38.5 0.3 reshape.50
  38.8 21.3 %all_to_all.11 = bf16[8,36,2048]{2,1,0:T(8,128)(2,1)S(1)} all-to-all(bf16[8,36,2048]{2,1,0:T(8,128)(2,1)S(1)} %reshape.50), channel_id=1, replica_groups=mesh['dp'=16,'expert'=8] {'expert'}, dimensions={0} | all-to-all | bytes 2359296 | tf_op jit(solution)/shard_map/all_to_all | solution.py:74
  60.1 1.1 reshape.51
  61.2 0.0 all-gather.9.cloned.1.call-update
  61.2 0.0 all-gather.13.cloned.1.call-start
  61.3 0.5 all-gather.13.cloned.1.call-update
  61.8 0.0 reduce-scatter.2.cloned.1.call-start
  61.8 10.0 %all-gather.7.cloned.1.call-done = bf16[1152,2048]{1,0:T(8,128)(2,1)} async-done(((bf16[288,2048]{1,0:T(8,128)(2,1)}), bf16[1152,2048]{1,0:T(8,128)(2,1)}) %all-gather.7.cloned.1.call-update) | async-done | bytes 4718608 | tf_op jit(solution)/shard_map/all_gather | solution.py:78
  71.8 47.7 %all-gather.11.cloned.1.call-done = bf16[1,1792,2048]{2,1,0:T(8,128)(2,1)} async-done(((bf16[1,448,2048]{2,1,0:T(8,128)(2,1)}), bf16[1,1792,2048]{2,1,0:T(8,128)(2,1)}) %all-gather.11.cloned.1.call-update) | async-done | bytes 7340048 | tf_op jit(solution)/shard_map/all_gather | solution.py:53
  119.6 14.7 %fusion.5 = f32[1152,1792]{1,0:T(8,128)} fusion(bf16[1152,2048]{1,0:T(8,128)(2,1)} %all-gather.7.cloned.1.call-done, bf16[1,1792,2048]{2,1,0:T(8,128)(2,1)} %all-gather.11.cloned.1.call-done), kind=kOutput, calls=%fused_computation.5 | convolution fusion | flops 8455716864 | bytes 20316160 | tf_op jit(solution)/shard_map/dot_general | solution.py:80
  134.2 22.1 %all-gather.9.cloned.1.call-done = bf16[1152,2048]{1,0:T(8,128)(2,1)} async-done(((bf16[288,2048]{1,0:T(8,128)(2,1)}), bf16[1152,2048]{1,0:T(8,128)(2,1)}) %all-gather.9.cloned.1.call-update) | async-done | bytes 4718608 | tf_op jit(solution)/shard_map/all_gather | solution.py:79
  156.4 47.6 %all-gather.13.cloned.1.call-done = bf16[1,1792,2048]{2,1,0:T(8,128)(2,1)} async-done(((bf16[1,448,2048]{2,1,0:T(8,128)(2,1)}), bf16[1,1792,2048]{2,1,0:T(8,128)(2,1)}) %all-gather.13.cloned.1.call-update) | async-done | bytes 7340048 | tf_op jit(solution)/shard_map/all_gather | solution.py:54
  204.0 28.2 %fusion.2 = bf16[1792,2048]{1,0:T(8,128)(2,1)} fusion(bf16[1152,2048]{1,0:T(8,128)(2,1)} %all-gather.9.cloned.1.call-done, bf16[1152,2048]{1,0:T(8,128)(2,1)} %all-gather.7.cloned.1.call-done, f32[1152,1792]{1,0:T(8,128)} %fusion.5, bf16[1,1792,2048]{2,1,0:T(8,128)(2,1)} %all-gather.13.cloned.1.call-done), kind=kOutput, calls=%fused_computation.3 | convolution fusion | flops 16927490048 | bytes 32374784 | tf_op jit(solution)/shard_map/dot_general | solution.py:87
  232.2 0.0 reduce-scatter.2.cloned.1.call-update
  232.2 44.5 %reduce-scatter.2.cloned.1.call-done = bf16[448,2048]{1,0:T(8,128)(2,1)} async-done(((bf16[1792,2048]{1,0:T(8,128)(2,1)}), bf16[448,2048]{1,0:T(8,128)(2,1)}) %reduce-scatter.2.cloned.1.call-update) | async-done | bytes 1835024 | tf_op jit(solution)/shard_map/reduce_scatter | solution.py:90
  276.7 0.0 copy-start.1
  276.7 9.9 %multiply_add_fusion = (f32[1,448,2048]{2,1,0:T(8,128)}, f32[1,448,2048]{2,1,0:T(8,128)}, f32[1,448,2048]{2,1,0:T(8,128)}) fusion(f32[1,448,2048]{2,1,0:T(8,128)} %param.16, f32[1,448,2048]{2,1,0:T(8,128)} %param.15, bf16[448,2048]{1,0:T(8,128)(2,1)} %reduce-scatter.2.cloned.1.call-done, f32[1,448,2048]{2,1,0:T(8,128)} %param.17), kind=kLoop, calls=%fused_computation.18 | loop fusion | flops 17432576 | bytes 23855104 | tf_op jit(solution)/shard_map/add | solution.py:99
  286.7 0.0 copy-done.1
  (3 shorter events, 0.0 us)
Async XLA Ops:
  7.2 4.5 %copy-start = (bf16[128,2048]{1,0:T(8,128)(2,1)S(1)}, bf16[128,2048]{1,0:T(8,128)(2,1)}, u32[]{:S(2)}) copy-start(bf16[128,2048]{1,0:T(8,128)(2,1)} %param.9) | copy-start | bytes 1572868
  7.2 64.7 %all-gather.7.cloned.1.call-start = ((), (), s32[]{:S(2)}) async-start(), calls=%async_computation.3 | async-start | bytes 5898240 | tf_op jit(solution)/shard_map/all_gather | solution.py:78
  12.4 25.6 %copy-start.2 = (bf16[128,2048]{1,0:T(8,128)(2,1)S(1)}, bf16[128,2048]{1,0:T(8,128)(2,1)}, u32[]{:S(2)}) copy-start(bf16[128,2048]{1,0:T(8,128)(2,1)} %param.10) | copy-start | bytes 1572868
  37.2 82.3 %all-gather.11.cloned.1.call-start = ((), (), s32[]{:S(2)}) async-start(), calls=%async_computation.6 | async-start | bytes 9175040 | tf_op jit(solution)/shard_map/all_gather | solution.py:53
  38.0 118.4 %all-gather.9.cloned.1.call-start = ((), (), s32[]{:S(2)}) async-start(), calls=%async_computation.4 | async-start | bytes 5898240 | tf_op jit(solution)/shard_map/all_gather | solution.py:79
  61.2 142.7 %all-gather.13.cloned.1.call-start = ((), (), s32[]{:S(2)}) async-start(), calls=%async_computation.7 | async-start | bytes 9175040 | tf_op jit(solution)/shard_map/all_gather | solution.py:54
  61.8 214.9 %reduce-scatter.2.cloned.1.call-start = ((), (), s32[]{:S(2)}) async-start(), calls=%async_computation.5 | async-start | bytes 9175040 | tf_op jit(solution)/shard_map/reduce_scatter | solution.py:90
  276.7 9.9 %copy-start.1 = (bf16[128,2048]{1,0:T(8,128)(2,1)S(1)}, bf16[128,2048]{1,0:T(8,128)(2,1)}, u32[]{:S(2)}) copy-start(bf16[128,2048]{1,0:T(8,128)(2,1)} %param.9) | copy-start | bytes 1572868
Sparse Core Ops, SparseCore 0:
  37.3 34.4 all-gather.6
  73.5 46.0 all-gather.10
  121.8 34.5 all-gather.8
  157.9 46.0 all-gather.12
  232.3 44.3 reduce-scatter.1

commit v2 on v1

v2 whole, which is shorter than its diff:
```python
import functools

import jax
import jax.numpy as jnp
from jax import lax
from jax.experimental import pallas as pl
from jax.experimental.pallas import tpu as pltpu
from jax.sharding import PartitionSpec as P

FF = 7168
TOPK = 2

beta_one = 0.9
beta_two = 0.95
learn_rate = 0.05
decay_rate = 0.1
step_count = 4.0
epsilon = 1e-08

SIDE = 4
CHUNKS = 4
MESH = pl.DeviceIdType.MESH
NT = (((1,), (1,)), ((), ()))


def dot(a, b):
    return jnp.dot(a, b, preferred_element_type=jnp.float32)


def exchange(
    experts,
    cap,
    tok_ref,
    cot_ref,
    ids_ref,
    share_ref,
    gate_ref,
    up_ref,
    out_ref,
    pack,
    land,
    rows,
    grads,
    weights,
    hid,
    hid_t,
    part,
    opp_in,
    dir_in,
    acc_in,
    own_sem,
    w_send,
    w_recv,
    a_send,
    a_recv,
    r_send,
    r_recv,
    opp_send,
    opp_recv,
    dir_send,
    dir_recv,
    acc_send,
    acc_recv,
):
    dp = lax.axis_index("dp")
    me = lax.axis_index("expert")
    core = me % 2
    hi, lo = dp // SIDE, dp % SIDE
    p = core * hi + (1 - core) * lo
    q = core * lo + (1 - core) * hi

    def peer(p_to, q_to, e_to):
        to = core * (p_to * SIDE + q_to) + (1 - core) * (q_to * SIDE + p_to)
        return {"dp": to, "expert": e_to}

    p_left, p_right, p_far = (p + 3) % SIDE, (p + 1) % SIDE, (p + 2) % SIDE
    q_left, q_right, q_far = (q + 3) % SIDE, (q + 1) % SIDE, (q + 2) % SIDE
    w_left, w_right = peer(p_left, q, me), peer(p_right, q, me)
    r_left, r_right = peer(p, q_left, me), peer(p, q_right, me)

    barrier = pltpu.get_barrier_semaphore()
    for to in (w_left, w_right, r_left, r_right):
        pl.semaphore_signal(barrier, inc=1, device_id=to, device_id_type=MESH)
    for i in range(1, experts):
        pl.semaphore_signal(
            barrier, inc=1, device_id=peer(p, q, (me + i) % experts), device_id_type=MESH
        )
    pl.semaphore_wait(barrier, 4 + experts - 1)

    def remote(src, dst, send, recv, to):
        return pltpu.make_async_remote_copy(
            src_ref=src, dst_ref=dst, send_sem=send, recv_sem=recv, device_id=to,
            device_id_type=MESH,
        )

    def weight_copy(i):
        if i == 0:
            return remote(gate_ref, weights.at[p, 0], w_send.at[0], w_recv.at[0], w_left)
        if i == 1:
            return remote(up_ref, weights.at[p, 1], w_send.at[1], w_recv.at[1], w_right)
        if i == 2:
            return remote(up_ref, weights.at[p, 1], w_send.at[2], w_recv.at[2], w_left)
        if i == 3:
            return remote(gate_ref, weights.at[p, 0], w_send.at[3], w_recv.at[3], w_right)
        if i == 4:
            ref = weights.at[p_right, 0]
            return remote(ref, ref, w_send.at[4], w_recv.at[4], w_left)
        ref = weights.at[p_left, 1]
        return remote(ref, ref, w_send.at[5], w_recv.at[5], w_right)

    for i in range(4):
        weight_copy(i).start()
    own_gate = pltpu.make_async_copy(gate_ref, weights.at[p, 0], own_sem.at[0])
    own_up = pltpu.make_async_copy(up_ref, weights.at[p, 1], own_sem.at[1])
    own_gate.start()
    own_up.start()

    toks = tok_ref.shape[0]
    number = lax.broadcasted_iota(jnp.int32, (experts, toks), 0)
    before = (
        lax.broadcasted_iota(jnp.int32, (toks, toks), 0)
        < lax.broadcasted_iota(jnp.int32, (toks, toks), 1)
    ).astype(jnp.bfloat16)
    id_a, id_b = ids_ref[0:1, :], ids_ref[1:2, :]
    hot_a = (number == id_a).astype(jnp.float32)
    hot_b = (number == id_b).astype(jnp.float32)
    count_a = dot(hot_a.astype(jnp.bfloat16), before)
    count_b = dot(hot_b.astype(jnp.bfloat16), before) + jnp.sum(hot_a, axis=1, keepdims=True)
    slot_a = jnp.sum(hot_a * count_a, axis=0, keepdims=True).astype(jnp.int32)
    slot_b = jnp.sum(hot_b * count_b, axis=0, keepdims=True).astype(jnp.int32)
    share = share_ref[...]
    line = lax.broadcasted_iota(jnp.int32, (2 * cap, toks), 0)

    def fill(i, carry):
        to = (me + i) % experts
        at_a = jnp.where(id_a == to, slot_a, -1 - 2 * cap)
        at_b = jnp.where(id_b == to, slot_b, -1 - 2 * cap)
        row_pick = ((line == at_a) | (line == at_b)).astype(jnp.float32).astype(jnp.bfloat16)
        low_a, low_b = line == at_a + cap, line == at_b + cap
        grad_pick = (low_a | low_b).astype(jnp.float32).astype(jnp.bfloat16)
        scale = jnp.sum(
            jnp.where(low_a, share, 0.0) + jnp.where(low_b, 1.0 - share, 0.0),
            axis=1,
            keepdims=True,
        )
        both = dot(row_pick, tok_ref[...]) + scale * dot(grad_pick, cot_ref[...])
        pack[to] = both.astype(jnp.bfloat16)
        return carry

    lax.fori_loop(0, experts, fill, 0)

    def route_copy(i):
        to = (me + i) % experts
        return remote(
            pack.at[to], land.at[me], a_send.at[i - 1], a_recv.at[i - 1], peer(p, q, to)
        )

    for i in range(1, experts):
        route_copy(i).start()
    land[me] = pack[me]

    weight_copy(0).wait_recv()
    weight_copy(4).start()
    weight_copy(1).wait_recv()
    weight_copy(5).start()

    for i in range(1, experts):
        route_copy(i).wait_recv()

    block = experts * cap
    wide = lax.broadcasted_iota(jnp.int32, (block, 2 * block), 1)
    deep = lax.broadcasted_iota(jnp.int32, (block, 2 * block), 0)
    source = jnp.floor((wide.astype(jnp.float32) + 0.5) * (1.0 / (2 * cap))).astype(jnp.int32)
    inside = wide - source * (2 * cap)
    row_from = jnp.where(inside < cap, source * cap + inside, -1)
    grad_from = jnp.where(inside >= cap, source * cap + inside - cap, -1)
    landed = land[...].reshape(2 * block, land.shape[2])
    pick = (deep == row_from).astype(jnp.float32).astype(jnp.bfloat16)
    rows[q] = dot(pick, landed).astype(jnp.bfloat16)
    pick = (deep == grad_from).astype(jnp.float32).astype(jnp.bfloat16)
    grads[q] = dot(pick, landed).astype(jnp.bfloat16)

    def row_copy(i):
        if i == 0:
            return remote(rows.at[q], rows.at[q], r_send.at[0], r_recv.at[0], r_left)
        if i == 1:
            return remote(grads.at[q], grads.at[q], r_send.at[1], r_recv.at[1], r_right)
        if i == 2:
            return remote(grads.at[q], grads.at[q], r_send.at[2], r_recv.at[2], r_left)
        if i == 3:
            return remote(rows.at[q], rows.at[q], r_send.at[3], r_recv.at[3], r_right)
        if i == 4:
            ref = rows.at[q_right]
            return remote(ref, ref, r_send.at[4], r_recv.at[4], r_left)
        ref = grads.at[q_left]
        return remote(ref, ref, r_send.at[5], r_recv.at[5], r_right)

    for i in range(4):
        row_copy(i).start()

    def forward(b, s):
        x = rows[b]
        gate = lax.dot_general(x, weights[s, 0], NT, preferred_element_type=jnp.float32)
        up = lax.dot_general(x, weights[s, 1], NT, preferred_element_type=jnp.float32)
        hid[s, b] = (gate / (1.0 + jnp.exp(-gate)) * up).astype(jnp.bfloat16)

    def forward_near(b):
        def step(i, carry):
            forward(b, (p + 3 + i) % SIDE)
            return carry

        lax.fori_loop(0, 3, step, 0)

    own_gate.wait()
    own_up.wait()
    weight_copy(2).wait_recv()
    weight_copy(3).wait_recv()
    forward_near(q)
    row_copy(0).wait_recv()
    row_copy(4).start()
    row_copy(1).wait_recv()
    row_copy(5).start()
    forward_near(q_right)
    row_copy(3).wait_recv()
    forward_near(q_left)
    weight_copy(4).wait_recv()
    weight_copy(5).wait_recv()

    def step_far(i, carry):
        forward((q + 3 + i) % SIDE, p_far)
        return carry

    lax.fori_loop(0, 3, step_far, 0)
    row_copy(2).wait_recv()
    row_copy(4).wait_recv()
    row_copy(5).wait_recv()

    def far_copy(c):
        return remote(
            part.at[p_far, c], opp_in.at[c], opp_send.at[c], opp_recv.at[c],
            peer((p + 3 + 2 * (c // 2)) % SIDE, q, me),
        )

    def near_copy(c):
        to = (p + 1 + 2 * (c // 2)) % SIDE
        return remote(
            part.at[to, c], dir_in.at[c], dir_send.at[c], dir_recv.at[c], peer(to, q, me)
        )

    def sum_copy(c):
        to = (p + 3 + 2 * (c // 2)) % SIDE
        return remote(
            part.at[to, c], acc_in.at[c], acc_send.at[c], acc_recv.at[c], peer(to, q, me)
        )

    all_rows = SIDE * block
    full = hid.shape[3]
    chunk = part.shape[3]

    def backward(s, first, send):
        forward(q_far, s)
        hid_t[...] = hid[s].reshape(all_rows, full).T

        def step(j, carry):
            c = (first + j) % CHUNKS
            at = pl.ds(pl.multiple_of(c * chunk, chunk), chunk)
            grad = grads[:, :, at].reshape(all_rows, chunk)
            part[s, c] = dot(hid_t[...], grad).astype(jnp.bfloat16)
            return carry

        lax.fori_loop(0, CHUNKS, step, 0)
        for c in send:
            if s is p_far:
                far_copy(c).start()
            else:
                near_copy(c).start()

    backward(p_far, 0, (0, 2, 1, 3))
    backward(p_left, 2, (2, 3))
    backward(p_right, 0, (0, 1))
    for c in (0, 2, 1, 3):
        far_copy(c).wait_recv()
        to = (p + 3 + 2 * (c // 2)) % SIDE
        part[to, c] = (
            part[to, c].astype(jnp.float32) + opp_in[c].astype(jnp.float32)
        ).astype(jnp.bfloat16)
        sum_copy(c).start()
    backward(p, 0, ())
    for c in (0, 2, 1, 3):
        near_copy(c).wait_recv()
        sum_copy(c).wait_recv()
        out_ref[:, c * chunk : (c + 1) * chunk] = (
            part[p, c].astype(jnp.float32)
            + dir_in[c].astype(jnp.float32)
            + acc_in[c].astype(jnp.float32)
        )
    for i in range(6):
        weight_copy(i).wait_send()
        row_copy(i).wait_send()
    for i in range(1, experts):
        route_copy(i).wait_send()
    for c in range(CHUNKS):
        far_copy(c).wait_send()
        near_copy(c).wait_send()
        sum_copy(c).wait_send()


def shards(
    tokens,
    cotangent,
    expert_ids,
    route_share,
    gate_proj,
    up_proj,
    down_anchor,
    down_average,
    down_moment,
):
    experts = lax.axis_size("expert")
    toks, width = tokens.shape
    cap = toks * TOPK // experts * 9 // 8
    block = experts * cap
    full = gate_proj.shape[1]
    chunk = width // CHUNKS
    bf16 = jnp.bfloat16
    vmem = pl.BlockSpec(memory_space=pltpu.VMEM)
    hbm = pl.BlockSpec(memory_space=pl.ANY)
    dma = pltpu.SemaphoreType.DMA
    gradient = pl.pallas_call(
        functools.partial(exchange, experts, cap),
        out_shape=jax.ShapeDtypeStruct((full, width), jnp.float32),
        in_specs=[vmem, vmem, vmem, vmem, hbm, hbm],
        out_specs=vmem,
        scratch_shapes=[
            pltpu.VMEM((experts, 2 * cap, width), bf16),
            pltpu.VMEM((experts, 2 * cap, width), bf16),
            pltpu.VMEM((SIDE, block, width), bf16),
            pltpu.VMEM((SIDE, block, width), bf16),
            pltpu.VMEM((SIDE, 2, full, width), bf16),
            pltpu.VMEM((SIDE, SIDE, block, full), bf16),
            pltpu.VMEM((full, SIDE * block), bf16),
            pltpu.VMEM((SIDE, CHUNKS, full, chunk), bf16),
            pltpu.VMEM((CHUNKS, full, chunk), bf16),
            pltpu.VMEM((CHUNKS, full, chunk), bf16),
            pltpu.VMEM((CHUNKS, full, chunk), bf16),
            dma((2,)),
            dma((6,)),
            dma((6,)),
            dma((experts - 1,)),
            dma((experts - 1,)),
            dma((6,)),
            dma((6,)),
            dma((CHUNKS,)),
            dma((CHUNKS,)),
            dma((CHUNKS,)),
            dma((CHUNKS,)),
            dma((CHUNKS,)),
            dma((CHUNKS,)),
        ],
        compiler_params=pltpu.CompilerParams(
            collective_id=0, has_side_effects=True, vmem_limit_bytes=67043328
        ),
        name="exchange",
    )(tokens, cotangent, expert_ids.T, route_share[None], gate_proj[0], up_proj[0])
    gradient = gradient[None] * FF ** (-0.5)
    bias_two = 1.0 - beta_two**step_count
    eval_point = (1.0 - beta_one) * down_anchor + beta_one * down_average
    second_moment = beta_two * down_moment + (1.0 - beta_two) * gradient * gradient
    update_dir = gradient / (jnp.sqrt(second_moment / bias_two) + epsilon) + decay_rate * eval_point
    new_anchor = down_anchor - learn_rate * update_dir
    new_average = (1.0 - 1.0 / step_count) * down_average + 1.0 / step_count * new_anchor
    return (new_anchor, new_average, second_moment)


def solution(mesh):
    placed = (
        P(("dp", "expert"), None),
        P(("dp", "expert"), None),
        P(("dp", "expert"), None),
        P(("dp", "expert")),
        P("expert", "dp", None),
        P("expert", "dp", None),
        P("expert", "dp", None),
        P("expert", "dp", None),
        P("expert", "dp", None),
    )
    return jax.shard_map(
        shards,
        mesh=mesh,
        in_specs=placed,
        out_specs=(P("expert", "dp", None), P("expert", "dp", None), P("expert", "dp", None)),
        check_vma=False,
    )
```

time: 293 us -> 160 us (0.55)
  waiting for transfers between devices: 173 us -> 0 us
  Pallas kernels: 0 us -> 149 us
  blocking collectives: 44.9 us -> 0 us
  matrix products: 43.8 us -> 0 us
  between operations: 13.9 us -> 0.64 us
  local copies, waits for them, and re-layouts: 4.37 us -> 0 us
    pallas_call x0 -> x1, Pallas kernels: none -> 149 us  [shards(): pl.pallas_call(functools.partial(exchange, experts, cap), out_shape=jax.S...]
    all_gather x4 -> x0, waiting for transfers between devices: 127 us -> none  [the longest x1 47.7 us: shards(): lax.all_gather(gate_proj[0], BOTH, axis=0, tiled=True, axis_index_groups=...]
    all_to_all x2 -> x0, blocking collectives: 44.9 us -> none  [the longest x1 23.6 us: shards(): lax.all_to_all(send_rows.reshape(experts_all, capacity, width), 'expert',...]
    reduce_scatter x1 -> x0, waiting for transfers between devices: 44.5 us -> none  [shards(): lax.psum_scatter(part, BOTH, scatter_dimension=0, tiled=True, axis_index_...]
    dot_general x4 -> x0, matrix products: 43.8 us -> none  [the longest x1 28.2 us: shards(): lax.dot_general(hidden, grad_all, (((0,), (0,)), ((), ())), preferred_ele...]
  transfers between devices with their start and end apart: 5 -> 0, of which waited for: 5 -> 0; matrix products, arithmetic and copies ran while one was open for 6% -> 0% of each run, Pallas kernels for 0% -> 0%
where the time goes in v2:
time: 160 us; the launch traced here: 159 us
  Pallas kernels  149 us (93%)
  other arithmetic  10.3 us (6%)
    pallas_call x1, Pallas kernels, shards(): pl.pallas_call(functools.partial(exchange, experts, cap), out_shape=jax.S...  149 us
    add x1, other arithmetic, shards(): (1.0 - 1.0 / step_count) * down_average + 1.0 / step_count * new_anchor  10.3 us

profile of v2, /device:TPU:1, one launch (start us, length us, event | category | flops | bytes accessed | tf_op | source)
XLA Modules:
  0.0 159.5 jit_solution(1155046163104326591)
XLA Ops:
  0.6 148.6 %exchange.1 = f32[448,2048]{1,0:T(8,128)} custom-call(bf16[128,2048]{1,0:T(8,128)(2,1)} %tok_ref.1, bf16[128,2048]{1,0:T(8,128)(2,1)} %cot_ref.1, s32[2,128]{1,0:T(2,128)} %bitcast.18, f32[1,128]{1,0:T(1,128)} %bitcast.19, bf16[448,2048]{1,0:T(8,128)(2,1)} %bitcast.16, bf16[448,2048]{1,0:T(8,128)(2,1)} %bitcast.17), custom_call_target="tpu_custom_call" | custom-call | tf_op jit(solution)/shard_map/exchange/pallas_call | solution.py:329
  149.2 10.3 %multiply_add_fusion = (f32[1,448,2048]{2,1,0:T(8,128)}, f32[1,448,2048]{2,1,0:T(8,128)}, f32[1,448,2048]{2,1,0:T(8,128)}) fusion(f32[1,448,2048]{2,1,0:T(8,128)} %param.16, f32[1,448,2048]{2,1,0:T(8,128)} %param.15, f32[448,2048]{1,0:T(8,128)} %exchange.1, f32[1,448,2048]{2,1,0:T(8,128)} %param.17), kind=kLoop, calls=%fused_computation.5 | loop fusion | flops 16515072 | bytes 25690112 | tf_op jit(solution)/shard_map/add | solution.py:371

commit v3 on v2

--- a/solution.py
+++ b/solution.py
@@ -48,6 +48,7 @@
     opp_in,
     dir_in,
     acc_in,
+    total,
     own_sem,
     w_send,
     w_recv,
@@ -85,7 +86,6 @@
         pl.semaphore_signal(
             barrier, inc=1, device_id=peer(p, q, (me + i) % experts), device_id_type=MESH
         )
-    pl.semaphore_wait(barrier, 4 + experts - 1)
 
     def remote(src, dst, send, recv, to):
         return pltpu.make_async_remote_copy(
@@ -108,8 +108,6 @@
         ref = weights.at[p_left, 1]
         return remote(ref, ref, w_send.at[5], w_recv.at[5], w_right)
 
-    for i in range(4):
-        weight_copy(i).start()
     own_gate = pltpu.make_async_copy(gate_ref, weights.at[p, 0], own_sem.at[0])
     own_up = pltpu.make_async_copy(up_ref, weights.at[p, 1], own_sem.at[1])
     own_gate.start()
@@ -148,6 +146,9 @@
         return carry
 
     lax.fori_loop(0, experts, fill, 0)
+    pl.semaphore_wait(barrier, 4 + experts - 1)
+    for i in range(4):
+        weight_copy(i).start()
 
     def route_copy(i):
         to = (me + i) % experts
@@ -158,11 +159,6 @@
     for i in range(1, experts):
         route_copy(i).start()
     land[me] = pack[me]
-
-    weight_copy(0).wait_recv()
-    weight_copy(4).start()
-    weight_copy(1).wait_recv()
-    weight_copy(5).start()
 
     for i in range(1, experts):
         route_copy(i).wait_recv()
@@ -189,11 +185,12 @@
             return remote(grads.at[q], grads.at[q], r_send.at[2], r_recv.at[2], r_left)
         if i == 3:
             return remote(rows.at[q], rows.at[q], r_send.at[3], r_recv.at[3], r_right)
-        if i == 4:
-            ref = rows.at[q_right]
-            return remote(ref, ref, r_send.at[4], r_recv.at[4], r_left)
-        ref = grads.at[q_left]
-        return remote(ref, ref, r_send.at[5], r_recv.at[5], r_right)
+        half = pl.ds((i - 4) // 2 * (block // 2), block // 2)
+        if i % 2 == 0:
+            ref = rows.at[q_right, half]
+            return remote(ref, ref, r_send.at[i], r_recv.at[i], r_left)
+        ref = grads.at[q_left, half]
+        return remote(ref, ref, r_send.at[i], r_recv.at[i], r_right)
 
     for i in range(4):
         row_copy(i).start()
@@ -213,89 +210,125 @@
 
     own_gate.wait()
     own_up.wait()
-    weight_copy(2).wait_recv()
-    weight_copy(3).wait_recv()
+    for i in range(4):
+        weight_copy(i).wait_recv()
     forward_near(q)
     row_copy(0).wait_recv()
     row_copy(4).start()
+    row_copy(6).start()
     row_copy(1).wait_recv()
     row_copy(5).start()
+    row_copy(7).start()
     forward_near(q_right)
     row_copy(3).wait_recv()
     forward_near(q_left)
-    weight_copy(4).wait_recv()
-    weight_copy(5).wait_recv()
-
-    def step_far(i, carry):
-        forward((q + 3 + i) % SIDE, p_far)
-        return carry
-
-    lax.fori_loop(0, 3, step_far, 0)
     row_copy(2).wait_recv()
     row_copy(4).wait_recv()
+    weight_copy(4).start()
     row_copy(5).wait_recv()
+    weight_copy(5).start()
+    row_copy(6).wait_recv()
+    row_copy(7).wait_recv()
 
     def far_copy(c):
         return remote(
-            part.at[p_far, c], opp_in.at[c], opp_send.at[c], opp_recv.at[c],
+            part.at[1, c], opp_in.at[c], opp_send.at[c], opp_recv.at[c],
             peer((p + 3 + 2 * (c // 2)) % SIDE, q, me),
         )
 
     def near_copy(c):
         to = (p + 1 + 2 * (c // 2)) % SIDE
         return remote(
-            part.at[to, c], dir_in.at[c], dir_send.at[c], dir_recv.at[c], peer(to, q, me)
+            part.at[2 * (c // 2), c], dir_in.at[c], dir_send.at[c], dir_recv.at[c], peer(to, q, me)
         )
 
     def sum_copy(c):
         to = (p + 3 + 2 * (c // 2)) % SIDE
         return remote(
-            part.at[to, c], acc_in.at[c], acc_send.at[c], acc_recv.at[c], peer(to, q, me)
+            part.at[2 - 2 * (c // 2), c], acc_in.at[c], acc_send.at[c], acc_recv.at[c], peer(to, q, me)
         )
 
     all_rows = SIDE * block
     full = hid.shape[3]
     chunk = part.shape[3]
 
-    def backward(s, first, send):
+    def turn(s):
+        hid_t[...] = hid[s].reshape(all_rows, full).T
+
+    def backward(c):
+        at = pl.ds(pl.multiple_of(c * chunk, chunk), chunk)
+        return dot(hid_t[...], grads[:, :, at].reshape(all_rows, chunk))
+
+    def near_slice(first, s, place):
         forward(q_far, s)
-        hid_t[...] = hid[s].reshape(all_rows, full).T
+        turn(s)
 
         def step(j, carry):
             c = (first + j) % CHUNKS
-            at = pl.ds(pl.multiple_of(c * chunk, chunk), chunk)
-            grad = grads[:, :, at].reshape(all_rows, chunk)
-            part[s, c] = dot(hid_t[...], grad).astype(jnp.bfloat16)
+            part[place, c] = backward(c).astype(jnp.bfloat16)
+
+            @pl.when(j < 2)
+            def _():
+                near_copy(c).start()
+
             return carry
 
         lax.fori_loop(0, CHUNKS, step, 0)
-        for c in send:
-            if s is p_far:
-                far_copy(c).start()
-            else:
-                near_copy(c).start()
-
-    backward(p_far, 0, (0, 2, 1, 3))
-    backward(p_left, 2, (2, 3))
-    backward(p_right, 0, (0, 1))
-    for c in (0, 2, 1, 3):
+
+    near_slice(2, p_left, 2)
+    near_slice(0, p_right, 0)
+    forward(q_far, p)
+    turn(p)
+
+    def own_step(c, carry):
+        total[c] = backward(c)
+        return carry
+
+    lax.fori_loop(0, CHUNKS, own_step, 0)
+
+    weight_copy(4).wait_recv()
+    weight_copy(5).wait_recv()
+
+    def far_forward(b, carry):
+        forward(b, p_far)
+        return carry
+
+    lax.fori_loop(0, SIDE, far_forward, 0)
+    turn(p_far)
+
+    def far_step(j, carry):
+        c = (j % 2) * 2 + j // 2
+        part[1, c] = backward(c).astype(jnp.bfloat16)
+        far_copy(c).start()
+        return carry
+
+    lax.fori_loop(0, CHUNKS, far_step, 0)
+
+    def relay(j, carry):
+        c = (j % 2) * 2 + j // 2
         far_copy(c).wait_recv()
-        to = (p + 3 + 2 * (c // 2)) % SIDE
-        part[to, c] = (
-            part[to, c].astype(jnp.float32) + opp_in[c].astype(jnp.float32)
+        place = 2 - 2 * (c // 2)
+        part[place, c] = (
+            part[place, c].astype(jnp.float32) + opp_in[c].astype(jnp.float32)
         ).astype(jnp.bfloat16)
         sum_copy(c).start()
-    backward(p, 0, ())
+        return carry
+
+    lax.fori_loop(0, CHUNKS, relay, 0)
+
+    def result_copy(c):
+        return pltpu.make_async_copy(total.at[c], out_ref.at[c], own_sem.at[2 + c])
+
+    for c in range(CHUNKS):
+        near_copy(c).wait_recv()
+        total[c] = total[c] + dir_in[c].astype(jnp.float32)
     for c in (0, 2, 1, 3):
-        near_copy(c).wait_recv()
         sum_copy(c).wait_recv()
-        out_ref[:, c * chunk : (c + 1) * chunk] = (
-            part[p, c].astype(jnp.float32)
-            + dir_in[c].astype(jnp.float32)
-            + acc_in[c].astype(jnp.float32)
-        )
+        total[c] = total[c] + acc_in[c].astype(jnp.float32)
+        result_copy(c).start()
     for i in range(6):
         weight_copy(i).wait_send()
+    for i in range(8):
         row_copy(i).wait_send()
     for i in range(1, experts):
         route_copy(i).wait_send()
@@ -303,6 +336,80 @@
         far_copy(c).wait_send()
         near_copy(c).wait_send()
         sum_copy(c).wait_send()
+        result_copy(c).wait()
+
+
+STEP_ROWS = 64
+
+
+def update(
+    grad_hbm,
+    anchor_ref,
+    average_ref,
+    moment_hbm,
+    anchor_out,
+    average_out,
+    moment_out,
+    grad_ref,
+    moment_ref,
+    held,
+    in_sem,
+    sem,
+):
+    size = held.shape[2]
+    steps = anchor_ref.shape[0] // size
+    chunk = grad_hbm.shape[2]
+    bias_two = 1.0 - beta_two**step_count
+
+    def in_copy(k, i):
+        at = pl.ds(pl.multiple_of(i * size, size), size)
+        if k == 0:
+            return pltpu.make_async_copy(grad_hbm.at[0:CHUNKS, at], grad_ref.at[i], in_sem.at[0, i])
+        return pltpu.make_async_copy(moment_hbm.at[at], moment_ref.at[i], in_sem.at[1, i])
+
+    def out_copy(k, i):
+        at = pl.ds(pl.multiple_of(i * size, size), size)
+        out = (anchor_out, average_out, moment_out)[k]
+        return pltpu.make_async_copy(held.at[k, i % 2], out.at[at], sem.at[k, i % 2])
+
+    for i in range(steps):
+        for k in range(2):
+            in_copy(k, i).start()
+
+    def step(i, carry):
+        @pl.when(i >= 2)
+        def _():
+            for k in range(3):
+                out_copy(k, i - 2).wait()
+
+        at = pl.ds(pl.multiple_of(i * size, size), size)
+        slot = i % 2
+        for k in range(2):
+            in_copy(k, i).wait()
+        for c in range(CHUNKS):
+            cols = slice(c * chunk, (c + 1) * chunk)
+            gradient = grad_ref[i, c] * FF ** (-0.5)
+            anchor, average = anchor_ref[at, cols], average_ref[at, cols]
+            moment = beta_two * moment_ref[i, :, cols] + (1.0 - beta_two) * (gradient * gradient)
+            square = moment * (1.0 / bias_two)
+            root = square * lax.rsqrt(square)
+            kept = (1.0 - learn_rate * decay_rate * (1.0 - beta_one)) * anchor - (
+                learn_rate * decay_rate * beta_one
+            ) * average
+            new_anchor = kept - (learn_rate * gradient) / (root + epsilon)
+            held[0, slot, :, cols] = new_anchor
+            held[1, slot, :, cols] = (
+                1.0 - 1.0 / step_count
+            ) * average + 1.0 / step_count * new_anchor
+            held[2, slot, :, cols] = moment
+        for k in range(3):
+            out_copy(k, i).start()
+        return carry
+
+    lax.fori_loop(0, steps, step, 0)
+    for i in range(max(steps - 2, 0), steps):
+        for k in range(3):
+            out_copy(k, i).wait()
 
 
 def shards(
@@ -328,9 +435,9 @@
     dma = pltpu.SemaphoreType.DMA
     gradient = pl.pallas_call(
         functools.partial(exchange, experts, cap),
-        out_shape=jax.ShapeDtypeStruct((full, width), jnp.float32),
+        out_shape=jax.ShapeDtypeStruct((6 * CHUNKS, full, chunk), jnp.float32),
         in_specs=[vmem, vmem, vmem, vmem, hbm, hbm],
-        out_specs=vmem,
+        out_specs=hbm,
         scratch_shapes=[
             pltpu.VMEM((experts, 2 * cap, width), bf16),
             pltpu.VMEM((experts, 2 * cap, width), bf16),
@@ -339,17 +446,18 @@
             pltpu.VMEM((SIDE, 2, full, width), bf16),
             pltpu.VMEM((SIDE, SIDE, block, full), bf16),
             pltpu.VMEM((full, SIDE * block), bf16),
-            pltpu.VMEM((SIDE, CHUNKS, full, chunk), bf16),
+            pltpu.VMEM((SIDE - 1, CHUNKS, full, chunk), bf16),
             pltpu.VMEM((CHUNKS, full, chunk), bf16),
             pltpu.VMEM((CHUNKS, full, chunk), bf16),
             pltpu.VMEM((CHUNKS, full, chunk), bf16),
-            dma((2,)),
+            pltpu.VMEM((CHUNKS, full, chunk), jnp.float32),
+            dma((2 + CHUNKS,)),
             dma((6,)),
             dma((6,)),
             dma((experts - 1,)),
             dma((experts - 1,)),
-            dma((6,)),
-            dma((6,)),
+            dma((8,)),
+            dma((8,)),
             dma((CHUNKS,)),
             dma((CHUNKS,)),
             dma((CHUNKS,)),
@@ -358,18 +466,28 @@
             dma((CHUNKS,)),
         ],
         compiler_params=pltpu.CompilerParams(
-            collective_id=0, has_side_effects=True, vmem_limit_bytes=67043328
+            collective_id=0, has_side_effects=True, vmem_limit_bytes=54 * 1024 * 1024
         ),
         name="exchange",
     )(tokens, cotangent, expert_ids.T, route_share[None], gate_proj[0], up_proj[0])
-    gradient = gradient[None] * FF ** (-0.5)
-    bias_two = 1.0 - beta_two**step_count
-    eval_point = (1.0 - beta_one) * down_anchor + beta_one * down_average
-    second_moment = beta_two * down_moment + (1.0 - beta_two) * gradient * gradient
-    update_dir = gradient / (jnp.sqrt(second_moment / bias_two) + epsilon) + decay_rate * eval_point
-    new_anchor = down_anchor - learn_rate * update_dir
-    new_average = (1.0 - 1.0 / step_count) * down_average + 1.0 / step_count * new_anchor
-    return (new_anchor, new_average, second_moment)
+    size = STEP_ROWS if full % STEP_ROWS == 0 else full
+    whole = jax.ShapeDtypeStruct((full, width), jnp.float32)
+    outs = pl.pallas_call(
+        update,
+        out_shape=(whole, whole, whole),
+        in_specs=[hbm, vmem, vmem, hbm],
+        out_specs=(hbm, hbm, hbm),
+        scratch_shapes=[
+            pltpu.VMEM((full // size, CHUNKS, size, chunk), jnp.float32),
+            pltpu.VMEM((full // size, size, width), jnp.float32),
+            pltpu.VMEM((3, 2, size, width), jnp.float32),
+            dma((2, full // size)),
+            dma((3, 2)),
+        ],
+        compiler_params=pltpu.CompilerParams(vmem_limit_bytes=44 * 1024 * 1024),
+        name="update",
+    )(gradient, down_anchor[0], down_average[0], down_moment[0])
+    return tuple(out[None] for out in outs)
 
 
 def solution(mesh):

time: 160 us -> 149 us (0.931)
  other arithmetic: 10.3 us -> 0 us
    add x1 -> x0, other arithmetic: 10.3 us -> none  [shards(): (1.0 - 1.0 / step_count) * down_average + 1.0 / step_count * new_anchor]
    pallas_call x1, Pallas kernels: 149 us -> 140 us  [shards(): pl.pallas_call(functools.partial(exchange, experts, cap), out_shape=jax.S...]
    pallas_call x0 -> x1, Pallas kernels: none -> 7.45 us  [shards(): pl.pallas_call(update, out_shape=(whole, whole, whole), in_specs=[hbm, vm...]
where the time goes in v3:
time: 149 us
  Pallas kernels  148 us (99%)
    pallas_call x1, Pallas kernels, shards(): pl.pallas_call(functools.partial(exchange, experts, cap), out_shape=jax.S...  140 us
    pallas_call x1, Pallas kernels, shards(): pl.pallas_call(update, out_shape=(whole, whole, whole), in_specs=[hbm, vm...  7.45 us

profile of v3, /device:TPU:1, one launch (start us, length us, event | category | flops | bytes accessed | tf_op | source)
XLA Modules:
  0.0 148.6 jit_solution(3441104167376563445)
XLA Ops:
  0.6 0.0 copy-start
  0.6 0.0 copy-start.1
  0.7 140.4 %exchange.1.grad_hbm = f32[24,448,512]{2,1,0:T(8,128)} custom-call(bf16[128,2048]{1,0:T(8,128)(2,1)} %tok_ref.1, bf16[128,2048]{1,0:T(8,128)(2,1)} %cot_ref.1, s32[2,128]{1,0:T(2,128)} %bitcast.15, f32[1,128]{1,0:T(1,128)} %bitcast.16, bf16[448,2048]{1,0:T(8,128)(2,1)} %bitcast.13, bf16[448,2048]{1,0:T(8,128)(2,1)} %bitcast.14), custom_call_target="tpu_custom_call" | custom-call | tf_op jit(solution)/shard_map/exchange/pallas_call | solution.py:436
  141.1 0.0 copy-done
  141.1 0.0 copy-done.1
  141.1 7.5 %update.1 = (f32[448,2048]{1,0:T(8,128)}, f32[448,2048]{1,0:T(8,128)}, f32[448,2048]{1,0:T(8,128)}) custom-call(f32[24,448,512]{2,1,0:T(8,128)} %exchange.1.grad_hbm, f32[448,2048]{1,0:T(8,128)S(1)} %bitcast.10, f32[448,2048]{1,0:T(8,128)S(1)} %bitcast.11, f32[448,2048]{1,0:T(8,128)} %bitcast.12), custom_call_target="tpu_custom_call" | custom-call | tf_op jit(solution)/shard_map/update/pallas_call | solution.py:475
Async XLA Ops:
  0.6 140.4 %copy-start = (f32[1,448,2048]{2,1,0:T(8,128)S(1)}, f32[1,448,2048]{2,1,0:T(8,128)}, u32[]{:S(2)}) copy-start(f32[1,448,2048]{2,1,0:T(8,128)} %param.15) | copy-start | bytes 11010052
  0.6 140.4 %copy-start.1 = (f32[1,448,2048]{2,1,0:T(8,128)S(1)}, f32[1,448,2048]{2,1,0:T(8,128)}, u32[]{:S(2)}) copy-start(f32[1,448,2048]{2,1,0:T(8,128)} %param.16) | copy-start | bytes 11010052

commit v4 on v3

--- a/solution.py
+++ b/solution.py
@@ -30,13 +30,17 @@
 def exchange(
     experts,
     cap,
+    tok_hbm,
+    cot_hbm,
+    ids_hbm,
+    share_hbm,
+    gate_ref,
+    up_ref,
+    out_ref,
     tok_ref,
     cot_ref,
     ids_ref,
     share_ref,
-    gate_ref,
-    up_ref,
-    out_ref,
     pack,
     land,
     rows,
@@ -110,8 +114,27 @@
 
     own_gate = pltpu.make_async_copy(gate_ref, weights.at[p, 0], own_sem.at[0])
     own_up = pltpu.make_async_copy(up_ref, weights.at[p, 1], own_sem.at[1])
+    inputs = [
+        pltpu.make_async_copy(src, dst, own_sem.at[2 + CHUNKS + i])
+        for i, (src, dst) in enumerate(
+            (
+                (ids_hbm, ids_ref),
+                (share_hbm, share_ref),
+                (tok_hbm, tok_ref),
+                (cot_hbm, cot_ref),
+            )
+        )
+    ]
+    for copy in inputs:
+        copy.start()
+
+    pl.semaphore_wait(barrier, 4 + experts - 1)
+    for i in range(4):
+        weight_copy(i).start()
     own_gate.start()
     own_up.start()
+    for copy in inputs:
+        copy.wait()
 
     toks = tok_ref.shape[0]
     number = lax.broadcasted_iota(jnp.int32, (experts, toks), 0)
@@ -146,9 +169,6 @@
         return carry
 
     lax.fori_loop(0, experts, fill, 0)
-    pl.semaphore_wait(barrier, 4 + experts - 1)
-    for i in range(4):
-        weight_copy(i).start()
 
     def route_copy(i):
         to = (me + i) % experts
@@ -195,15 +215,15 @@
     for i in range(4):
         row_copy(i).start()
 
-    def forward(b, s):
+    def forward(b, s, slot):
         x = rows[b]
         gate = lax.dot_general(x, weights[s, 0], NT, preferred_element_type=jnp.float32)
         up = lax.dot_general(x, weights[s, 1], NT, preferred_element_type=jnp.float32)
-        hid[s, b] = (gate / (1.0 + jnp.exp(-gate)) * up).astype(jnp.bfloat16)
+        hid[slot, b] = (gate / (1.0 + jnp.exp(-gate)) * up).astype(jnp.bfloat16)
 
     def forward_near(b):
         def step(i, carry):
-            forward(b, (p + 3 + i) % SIDE)
+            forward(b, (p + 3 + i) % SIDE, i)
             return carry
 
         lax.fori_loop(0, 3, step, 0)
@@ -252,16 +272,16 @@
     full = hid.shape[3]
     chunk = part.shape[3]
 
-    def turn(s):
-        hid_t[...] = hid[s].reshape(all_rows, full).T
+    def turn(slot):
+        hid_t[...] = hid[slot].reshape(all_rows, full).T
 
     def backward(c):
         at = pl.ds(pl.multiple_of(c * chunk, chunk), chunk)
         return dot(hid_t[...], grads[:, :, at].reshape(all_rows, chunk))
 
-    def near_slice(first, s, place):
-        forward(q_far, s)
-        turn(s)
+    def near_slice(first, s, place, slot):
+        forward(q_far, s, slot)
+        turn(slot)
 
         def step(j, carry):
             c = (first + j) % CHUNKS
@@ -275,10 +295,10 @@
 
         lax.fori_loop(0, CHUNKS, step, 0)
 
-    near_slice(2, p_left, 2)
-    near_slice(0, p_right, 0)
-    forward(q_far, p)
-    turn(p)
+    near_slice(2, p_left, 2, 0)
+    near_slice(0, p_right, 0, 2)
+    forward(q_far, p, 1)
+    turn(1)
 
     def own_step(c, carry):
         total[c] = backward(c)
@@ -290,11 +310,11 @@
     weight_copy(5).wait_recv()
 
     def far_forward(b, carry):
-        forward(b, p_far)
+        forward(b, p_far, 0)
         return carry
 
     lax.fori_loop(0, SIDE, far_forward, 0)
-    turn(p_far)
+    turn(0)
 
     def far_step(j, carry):
         c = (j % 2) * 2 + j // 2
@@ -370,20 +390,14 @@
     def out_copy(k, i):
         at = pl.ds(pl.multiple_of(i * size, size), size)
         out = (anchor_out, average_out, moment_out)[k]
-        return pltpu.make_async_copy(held.at[k, i % 2], out.at[at], sem.at[k, i % 2])
+        return pltpu.make_async_copy(held.at[k, i], out.at[at], sem.at[k, i])
 
     for i in range(steps):
         for k in range(2):
             in_copy(k, i).start()
 
     def step(i, carry):
-        @pl.when(i >= 2)
-        def _():
-            for k in range(3):
-                out_copy(k, i - 2).wait()
-
         at = pl.ds(pl.multiple_of(i * size, size), size)
-        slot = i % 2
         for k in range(2):
             in_copy(k, i).wait()
         for c in range(CHUNKS):
@@ -397,17 +411,17 @@
                 learn_rate * decay_rate * beta_one
             ) * average
             new_anchor = kept - (learn_rate * gradient) / (root + epsilon)
-            held[0, slot, :, cols] = new_anchor
-            held[1, slot, :, cols] = (
+            held[0, i, :, cols] = new_anchor
+            held[1, i, :, cols] = (
                 1.0 - 1.0 / step_count
             ) * average + 1.0 / step_count * new_anchor
-            held[2, slot, :, cols] = moment
+            held[2, i, :, cols] = moment
         for k in range(3):
             out_copy(k, i).start()
         return carry
 
     lax.fori_loop(0, steps, step, 0)
-    for i in range(max(steps - 2, 0), steps):
+    for i in range(steps):
         for k in range(3):
             out_copy(k, i).wait()
 
@@ -436,22 +450,26 @@
     gradient = pl.pallas_call(
         functools.partial(exchange, experts, cap),
         out_shape=jax.ShapeDtypeStruct((6 * CHUNKS, full, chunk), jnp.float32),
-        in_specs=[vmem, vmem, vmem, vmem, hbm, hbm],
+        in_specs=[hbm] * 6,
         out_specs=hbm,
         scratch_shapes=[
+            pltpu.VMEM((toks, width), bf16),
+            pltpu.VMEM((toks, width), bf16),
+            pltpu.VMEM((TOPK, toks), jnp.int32),
+            pltpu.VMEM((1, toks), jnp.float32),
             pltpu.VMEM((experts, 2 * cap, width), bf16),
             pltpu.VMEM((experts, 2 * cap, width), bf16),
             pltpu.VMEM((SIDE, block, width), bf16),
             pltpu.VMEM((SIDE, block, width), bf16),
             pltpu.VMEM((SIDE, 2, full, width), bf16),
-            pltpu.VMEM((SIDE, SIDE, block, full), bf16),
+            pltpu.VMEM((SIDE - 1, SIDE, block, full), bf16),
             pltpu.VMEM((full, SIDE * block), bf16),
             pltpu.VMEM((SIDE - 1, CHUNKS, full, chunk), bf16),
             pltpu.VMEM((CHUNKS, full, chunk), bf16),
             pltpu.VMEM((CHUNKS, full, chunk), bf16),
             pltpu.VMEM((CHUNKS, full, chunk), bf16),
             pltpu.VMEM((CHUNKS, full, chunk), jnp.float32),
-            dma((2 + CHUNKS,)),
+            dma((6 + CHUNKS,)),
             dma((6,)),
             dma((6,)),
             dma((experts - 1,)),
@@ -480,9 +498,9 @@
         scratch_shapes=[
             pltpu.VMEM((full // size, CHUNKS, size, chunk), jnp.float32),
             pltpu.VMEM((full // size, size, width), jnp.float32),
-            pltpu.VMEM((3, 2, size, width), jnp.float32),
+            pltpu.VMEM((3, full // size, size, width), jnp.float32),
             dma((2, full // size)),
-            dma((3, 2)),
+            dma((3, full // size)),
         ],
         compiler_params=pltpu.CompilerParams(vmem_limit_bytes=44 * 1024 * 1024),
         name="update",

time: 149 us -> 146 us (0.980)
  Pallas kernels: 148 us -> 146 us
where the time goes in v4:
time: 146 us
  Pallas kernels  146 us (100%)
    pallas_call x1, Pallas kernels, shards(): pl.pallas_call(functools.partial(exchange, experts, cap), out_shape=jax.S...  139 us
    pallas_call x1, Pallas kernels, shards(): pl.pallas_call(update, out_shape=(whole, whole, whole), in_specs=[hbm, vm...  6.36 us

profile of v4, /device:TPU:1, one launch (start us, length us, event | category | flops | bytes accessed | tf_op | source)
XLA Modules:
  0.0 146.3 jit_solution(12285076204296970049)
XLA Ops:
  0.6 0.0 copy-start
  0.6 0.0 copy-start.1
  0.7 139.2 %exchange.1.grad_hbm = f32[24,448,512]{2,1,0:T(8,128)} custom-call(bf16[128,2048]{1,0:T(8,128)(2,1)} %tok_hbm.1, bf16[128,2048]{1,0:T(8,128)(2,1)} %cot_hbm.1, s32[2,128]{1,0:T(2,128)} %bitcast.15, f32[1,128]{1,0:T(1,128)} %bitcast.16, bf16[448,2048]{1,0:T(8,128)(2,1)} %bitcast.13, bf16[448,2048]{1,0:T(8,128)(2,1)} %bitcast.14), custom_call_target="tpu_custom_call" | custom-call | tf_op jit(solution)/shard_map/exchange/pallas_call | solution.py:450
  139.9 0.0 copy-done
  139.9 0.0 copy-done.1
  139.9 6.4 %update.1 = (f32[448,2048]{1,0:T(8,128)}, f32[448,2048]{1,0:T(8,128)}, f32[448,2048]{1,0:T(8,128)}) custom-call(f32[24,448,512]{2,1,0:T(8,128)} %exchange.1.grad_hbm, f32[448,2048]{1,0:T(8,128)S(1)} %bitcast.10, f32[448,2048]{1,0:T(8,128)S(1)} %bitcast.11, f32[448,2048]{1,0:T(8,128)} %bitcast.12), custom_call_target="tpu_custom_call" | custom-call | tf_op jit(solution)/shard_map/update/pallas_call | solution.py:493
Async XLA Ops:
  0.6 139.3 %copy-start = (f32[1,448,2048]{2,1,0:T(8,128)S(1)}, f32[1,448,2048]{2,1,0:T(8,128)}, u32[]{:S(2)}) copy-start(f32[1,448,2048]{2,1,0:T(8,128)} %param.15) | copy-start | bytes 11010052
  0.6 139.3 %copy-start.1 = (f32[1,448,2048]{2,1,0:T(8,128)S(1)}, f32[1,448,2048]{2,1,0:T(8,128)}, u32[]{:S(2)}) copy-start(f32[1,448,2048]{2,1,0:T(8,128)} %param.16) | copy-start | bytes 11010052

commit v5 on v4

--- a/solution.py
+++ b/solution.py
@@ -359,7 +359,7 @@
         result_copy(c).wait()
 
 
-STEP_ROWS = 64
+STEP_ROWS = 32
 
 
 def update(

time: 146 us -> 147 us (level)
  no operation moved by 1% of the time
where the time goes in v5:
time: 147 us
  Pallas kernels  146 us (99%)
    pallas_call x1, Pallas kernels, shards(): pl.pallas_call(functools.partial(exchange, experts, cap), out_shape=jax.S...  139 us
    pallas_call x1, Pallas kernels, shards(): pl.pallas_call(update, out_shape=(whole, whole, whole), in_specs=[hbm, vm...  7.03 us

profile of v5, /device:TPU:1, one launch (start us, length us, event | category | flops | bytes accessed | tf_op | source)
XLA Modules:
  0.0 146.9 jit_solution(4924978574482245530)
XLA Ops:
  0.6 0.0 copy-start
  0.6 0.0 copy-start.1
  0.7 139.2 %exchange.1.grad_hbm = f32[24,448,512]{2,1,0:T(8,128)} custom-call(bf16[128,2048]{1,0:T(8,128)(2,1)} %tok_hbm.1, bf16[128,2048]{1,0:T(8,128)(2,1)} %cot_hbm.1, s32[2,128]{1,0:T(2,128)} %bitcast.15, f32[1,128]{1,0:T(1,128)} %bitcast.16, bf16[448,2048]{1,0:T(8,128)(2,1)} %bitcast.13, bf16[448,2048]{1,0:T(8,128)(2,1)} %bitcast.14), custom_call_target="tpu_custom_call" | custom-call | tf_op jit(solution)/shard_map/exchange/pallas_call | solution.py:450
  139.9 0.0 copy-done
  139.9 0.0 copy-done.1
  139.9 7.0 %update.1 = (f32[448,2048]{1,0:T(8,128)}, f32[448,2048]{1,0:T(8,128)}, f32[448,2048]{1,0:T(8,128)}) custom-call(f32[24,448,512]{2,1,0:T(8,128)} %exchange.1.grad_hbm, f32[448,2048]{1,0:T(8,128)S(1)} %bitcast.10, f32[448,2048]{1,0:T(8,128)S(1)} %bitcast.11, f32[448,2048]{1,0:T(8,128)} %bitcast.12), custom_call_target="tpu_custom_call" | custom-call | tf_op jit(solution)/shard_map/update/pallas_call | solution.py:493
Async XLA Ops:
  0.6 139.3 %copy-start = (f32[1,448,2048]{2,1,0:T(8,128)S(1)}, f32[1,448,2048]{2,1,0:T(8,128)}, u32[]{:S(2)}) copy-start(f32[1,448,2048]{2,1,0:T(8,128)} %param.15) | copy-start | bytes 11010052
  0.6 139.3 %copy-start.1 = (f32[1,448,2048]{2,1,0:T(8,128)S(1)}, f32[1,448,2048]{2,1,0:T(8,128)}, u32[]{:S(2)}) copy-start(f32[1,448,2048]{2,1,0:T(8,128)} %param.16) | copy-start | bytes 11010052
